TPU v7x, 16 devices: a whole 2x2x2 slice. The times are simulated.
16 devices in a mesh: rep: 1, dp: 16 (over x, y, z, core).
Axes of the slice: x: 2, y: 2, z: 2, core: 2. Of those that a mesh axis runs over, the one named last changes fastest.
Arguments:
- a: bfloat16 [16, 4, 4096, 1280], P(('rep', 'dp'))
- g: bfloat16 [16, 4, 4096, 5120], P(('rep', 'dp'))
Outputs:
- output: bfloat16 [4, 1280, 5120], P('rep')
All inputs are finite; a program needn't handle non-finite values.
Results may differ from a plain program's by a relative error of at most 0.012.
Values are sent between devices in bfloat16 or wider.
A program may use at most 2 GiB of HBM per device.

v0:
```python
import jax
import jax.numpy as jnp


def solution(mesh):
    groups = mesh.shape["rep"]

    def step(a, g):
        a, g = (t.reshape(groups, -1, *t.shape[1:]) for t in (a, g))
        sums = jnp.einsum("rsntd,rsntf->rndf", a, g, preferred_element_type=jnp.float32)
        return sums.astype(jnp.bfloat16).reshape(-1, *sums.shape[2:])

    return step
```

profile of v0, /device:TPU:0, one launch (start us, length us, event | category | flops | bytes accessed | tf_op | source)
XLA Modules:
  0.0 1175.8 jit_solution(12631536856026246376)
XLA Ops:
  0.0 234.6 %fusion = f32[4,1280,5120]{2,1,0:T(8,128)} fusion(bf16[1,4,4096,5120]{3,2,1,0:T(8,128)(2,1)} %param.1, bf16[1,4,4096,1280]{3,2,1,0:T(8,128)(2,1)} %param), kind=kOutput, calls=%fused_computation | convolution fusion | flops 214748364800 | bytes 314572800 | tf_op jit(solution)/rsntd,rsntf->rndf/dot_general | solution.py:10
  234.6 941.1 %all-reduce.2 = bf16[4,1280,5120]{2,1,0:T(8,128)(2,1)} all-reduce(f32[4,1280,5120]{2,1,0:T(8,128)} %fusion), channel_id=1, replica_groups=mesh['axis_0'=16] {'axis_0'}, use_global_device_ids=true, to_apply=%add.clone | all-reduce | flops 26214400 | bytes 157286400 | tf_op jit(solution)/rsntd,rsntf->rndf/dot_general | solution.py:10
where the time goes:
time: 1180 us
  blocking collectives  941 us (80%)
  matrix products  235 us (20%)
    dot_general x1, blocking collectives, step(): jnp.einsum('rsntd,rsntf->rndf', a, g, preferred_element_type=jnp.float32)  941 us
    dot_general x1, matrix products, step(): jnp.einsum('rsntd,rsntf->rndf', a, g, preferred_element_type=jnp.float32)  235 us

commit v1 on v0

v1 whole, which is shorter than its diff:
```python
import jax
import jax.numpy as jnp
from jax import lax
from jax.experimental import pallas as pl
from jax.experimental.pallas import tpu as pltpu
from jax.sharding import PartitionSpec as P

MESH = pl.DeviceIdType.MESH
W = 256
K = 256
LAG = {1: 2, 2: 5, 3: 7, 4: 9, 5: 11, 6: 14, 7: 17, 8: 19, 9: 21}
SPARE = LAG[9] - LAG[4] + 3


def kernel(shape, a, g, out, at, a_in, g_in, acc, give, take, keep1, keep2, keep3, s1, s2, s3, r1, r2, r3, whole,
           a_sem, g_sem, o_sem, d_send, d_recv, rs_send, rs_recv, ag_send, ag_recv):
    mats, tokens, rows, cols = shape
    half = rows // 2
    per = cols // W
    units = mats * per
    chunks = tokens // K
    me = lax.axis_index("dp")
    core = me % 2
    bits = ((me // 8) % 2, (me // 4) % 2, (me // 2) % 2)

    def pick(j, x, y, z):
        return jnp.where(j == 0, x, jnp.where(j == 1, y, z))

    def route(v, s):
        j = lax.rem(v + s, 3)
        bit = pick(j, *bits)
        return bit, me + pick(j, 8, 4, 2) * (1 - 2 * bit)

    other = me + 1 - 2 * core

    def remote(src, dst, send, recv, to):
        return pltpu.make_async_remote_copy(src_ref=src, dst_ref=dst, send_sem=send, recv_sem=recv,
                                            device_id={"dp": to}, device_id_type=MESH)

    def aligned(x, n):
        return pl.multiple_of(x, n)

    def g_copy(i):
        n, j = i // (per // 2), lax.rem(i, per // 2)
        return pltpu.make_async_copy(g.at[0, n, :, pl.ds(aligned(j * 2 * W, 2 * W), 2 * W)],
                                     g_in.at[lax.rem(i, 2)], g_sem.at[lax.rem(i, 2)])

    def a_copy(n, c):
        return pltpu.make_async_copy(a.at[0, n, pl.ds(aligned(c * K, K), K), :], a_in.at[lax.rem(c, 2)], a_sem.at[lax.rem(c, 2)])

    def o_copy(v):
        n, j = v // per, lax.rem(v, per)
        slot = lax.rem(v, SPARE)
        return pltpu.make_async_copy(whole.at[slot], out.at[n, :, pl.ds(aligned(j * W, W), W)], o_sem.at[lax.rem(v, 3)])

    def flip(n, c):
        at[lax.rem(n, 2), :, pl.ds(aligned(c * K, K), K)] = a_in[lax.rem(c, 2)].T

    def swap(i):
        return remote(give, take.at[lax.rem(i, 3)], d_send.at[0], d_recv.at[lax.rem(i, 3)], other)

    def scatter(v, s):
        src, dst = ((s1, r1), (s2, r2), (s3, r3))[s]
        _, to = route(v, s)
        q = lax.rem(v, 6)
        return remote(src.at[lax.rem(v, 3)], dst.at[q], rs_send.at[s, lax.rem(v, 3)], rs_recv.at[s, q], to)

    def start_of(v, s):
        row, size = core * half, half
        for k in range(s):
            size //= 2
            row = row + route(v, k)[0] * size
        return row, size

    def gather(v, s):
        row, size = start_of(v, s + 1)
        _, to = route(v, s)
        q = lax.rem(v, 6)
        ref = whole.at[lax.rem(v, SPARE), pl.ds(aligned(row, rows // 16), size), :]
        return remote(ref, ref, ag_send.at[s, q], ag_recv.at[s, q], to)

    def share(v):
        q = lax.rem(v, 6)
        ref = whole.at[lax.rem(v, SPARE), pl.ds(aligned(core * half, half), half), :]
        return remote(ref, ref, ag_send.at[3, q], ag_recv.at[3, q], other)

    def add(v, s, mine, got, keep, send):
        bit, _ = route(v, s)
        n = got.shape[0] // 2
        yes, no = pl.ds(aligned(bit * n, n), n), pl.ds(aligned((1 - bit) * n, n), n)
        q = lax.rem(v, 3)
        send[q] = (mine[no, :] + got[no, :].astype(jnp.float32)).astype(jnp.bfloat16)
        keep[q] = mine[yes, :] + got[yes, :].astype(jnp.float32)

    def stages(t, h):
        def when(k, f):
            v = t - LAG[k]
            pl.when((v >= 0) & (v < units))(lambda: f(v))

        def nine(v):
            o_copy(v).wait()

        def eight(v):
            share(v).wait()
            o_copy(v).start()

        def seven(v):
            gather(v, 0).wait()
            share(v).start()

        def six(v):
            gather(v, 1).wait()
            gather(v, 0).start()

        def five(v):
            gather(v, 2).wait()
            gather(v, 1).start()

        def four(v):
            scatter(v, 2).wait()
            row, size = start_of(v, 3)
            done = keep3[lax.rem(v, 3)] + r3[lax.rem(v, 6)].astype(jnp.float32)
            whole[lax.rem(v, SPARE), pl.ds(aligned(row, rows // 16), size), :] = done.astype(jnp.bfloat16)
            gather(v, 2).start()

        def three(v):
            scatter(v, 1).wait()
            add(v, 2, keep2.at[lax.rem(v, 3)], r2.at[lax.rem(v, 6)], keep3, s3)
            scatter(v, 2).start()

        def two(v):
            scatter(v, 0).wait()
            add(v, 1, keep1.at[lax.rem(v, 3)], r1.at[lax.rem(v, 6)], keep2, s2)
            scatter(v, 1).start()

        def one(v):
            p = (h - LAG[1]) % 2
            i = v // 2
            if p == 0:
                swap(i).wait()
            c = slice(p * W, (p + 1) * W)
            add(v, 0, acc.at[:, c], take.at[lax.rem(i, 3), :, c], keep1, s1)
            scatter(v, 0).start()

        for k, f in ((9, nine), (8, eight), (7, seven), (6, six), (5, five), (4, four), (3, three), (2, two), (1, one)):
            when(k, f)

    g_copy(0).start()
    a_copy(0, 0).start()
    barrier = pltpu.get_barrier_semaphore()
    for b, bit in ((8, bits[0]), (4, bits[1]), (2, bits[2]), (1, core)):
        pl.semaphore_signal(barrier, inc=1, device_id={"dp": me + b * (1 - 2 * bit)}, device_id_type=MESH)
    pl.semaphore_wait(barrier, 4)

    def first(c, _):
        a_copy(0, c).wait()

        @pl.when(c + 1 < chunks)
        def _():
            a_copy(0, c + 1).start()
        flip(0, c)
        return 0

    lax.fori_loop(0, chunks, first, 0)

    def pair(i, _):
        n = (2 * i) // per
        for h in range(2):
            t = 2 * i + h
            c = lax.rem(t, per)
            ahead = (t < units - per) & (c < chunks)

            @pl.when(ahead)
            def _():
                a_copy(n + 1, c).start()

            stages(t, h)

            @pl.when(t < units)
            def _():
                if h == 0:
                    g_copy(i).wait()

                    @pl.when(i + 1 < units // 2)
                    def _():
                        g_copy(i + 1).start()
                side = core if h else 1 - core
                block = jnp.dot(at[lax.rem(n, 2), pl.ds(aligned(side * half, half), half), :], g_in[lax.rem(i, 2)],
                                preferred_element_type=jnp.float32)
                if h == 0:
                    give[...] = block.astype(jnp.bfloat16)
                    swap(i).start()
                else:
                    acc[...] = block

            @pl.when(ahead)
            def _():
                a_copy(n + 1, c).wait()
                flip(n + 1, c)
        return 0

    lax.fori_loop(0, (units + LAG[9] + 1 + 1) // 2, pair, 0)


def solution(mesh):
    def step(a, g):
        _, mats, tokens, rows = a.shape
        cols = g.shape[3]
        half = rows // 2
        bf, f32 = jnp.bfloat16, jnp.float32
        dma = pltpu.SemaphoreType.DMA
        return pl.pallas_call(
            lambda *refs: kernel((mats, tokens, rows, cols), *refs),
            out_shape=jax.ShapeDtypeStruct((mats, rows, cols), bf),
            in_specs=[pl.BlockSpec(memory_space=pl.ANY)] * 2,
            out_specs=pl.BlockSpec(memory_space=pl.ANY),
            scratch_shapes=[
                pltpu.VMEM((2, rows, tokens), bf),
                pltpu.VMEM((2, K, rows), bf),
                pltpu.VMEM((2, tokens, 2 * W), bf),
                pltpu.VMEM((half, 2 * W), f32),
                pltpu.VMEM((half, 2 * W), bf),
                pltpu.VMEM((3, half, 2 * W), bf),
                *[pltpu.VMEM((3, half // d, W), f32) for d in (2, 4, 8)],
                *[pltpu.VMEM((3, half // d, W), bf) for d in (2, 4, 8)],
                *[pltpu.VMEM((6, half // d, W), bf) for d in (2, 4, 8)],
                pltpu.VMEM((SPARE, rows, W), bf),
                dma((2,)), dma((2,)), dma((3,)), dma((1,)), dma((3,)),
                dma((3, 3)), dma((3, 6)), dma((4, 6)), dma((4, 6)),
            ],
            compiler_params=pltpu.CompilerParams(collective_id=0, has_side_effects=True, vmem_limit_bytes=63 * 2**20),
        )(a, g)

    return jax.shard_map(step, mesh=mesh, in_specs=(P(("rep", "dp")), P(("rep", "dp"))), out_specs=P("rep"), check_vma=False)
```

time: 1180 us -> 418 us (0.35)
  blocking collectives: 941 us -> 0 us
  Pallas kernels: 0 us -> 381 us
  matrix products: 235 us -> 0 us
  local copies, waits for them, and re-layouts: 0 us -> 35.7 us
    dot_general x1 -> x0, blocking collectives: 941 us -> none  [step(): jnp.einsum('rsntd,rsntf->rndf', a, g, preferred_element_type=jnp.float32)]
    pallas_call x0 -> x1, Pallas kernels: none -> 381 us  [step(): pl.pallas_call(lambda *refs: kernel((mats, tokens, rows, cols), *refs), o...]
    dot_general x1 -> x0, matrix products: 235 us -> none  [step(): jnp.einsum('rsntd,rsntf->rndf', a, g, preferred_element_type=jnp.float32)]
    unnamed x0 -> x1, local copies, waits for them, and re-layouts: none -> 35.7 us
where the time goes in v1:
time: 418 us; the launch traced here: 417 us
  Pallas kernels  381 us (91%)
  local copies, waits for them, and re-layouts  35.7 us (9%)
    pallas_call x1, Pallas kernels, step(): pl.pallas_call(lambda *refs: kernel((mats, tokens, rows, cols), *refs), o...  381 us
    unnamed x1, local copies, waits for them, and re-layouts  35.7 us

profile of v1, /device:TPU:0, one launch (start us, length us, event | category | flops | bytes accessed | tf_op | source)
XLA Modules:
  0.0 417.1 jit_solution(8322941577667867412)
XLA Ops:
  0.0 381.4 %shard_map.28 = bf16[4,1280,5120]{2,1,0:T(8,128)(2,1)} custom-call(bf16[1,4,4096,1280]{3,2,1,0:T(8,128)(2,1)} %refs_0_.1, bf16[1,4,4096,5120]{3,2,1,0:T(8,128)(2,1)} %refs_1_.1), custom_call_target="tpu_custom_call" | custom-call | tf_op jit(solution)/shard_map/pallas_call | solution.py:212
  381.5 35.7 %copy.4 = bf16[4,1280,5120]{2,1,0:T(8,128)(2,1)} copy(bf16[4,1280,5120]{2,1,0:T(8,128)(2,1)} %shard_map.28) | data formatting | bytes 104857600

commit v2 on v1

--- a/solution.py
+++ b/solution.py
@@ -8,17 +8,21 @@
 MESH = pl.DeviceIdType.MESH
 W = 256
 K = 256
-LAG = {1: 2, 2: 5, 3: 7, 4: 9, 5: 11, 6: 14, 7: 17, 8: 19, 9: 21}
-SPARE = LAG[9] - LAG[4] + 3
-
-
-def kernel(shape, a, g, out, at, a_in, g_in, acc, give, take, keep1, keep2, keep3, s1, s2, s3, r1, r2, r3, whole,
-           a_sem, g_sem, o_sem, d_send, d_recv, rs_send, rs_recv, ag_send, ag_recv):
+LAG = {1: 2, 2: 4, 3: 6, 4: 8, 5: 10, 6: 13, 7: 16, 8: 18, 9: 20}
+LANES = 16
+SPARE = 2 * LANES
+COLUMNS, UNITS, BLOCKS = 2, 3, 5
+ROWS = 4
+
+def kernel(shape, a, g, out, pool, a_in, acc, give, take, keep1, keep2, keep3, s1, s2, s3, r1, r2, r3,
+           a_sem, g_sem, o_sem, b_sem, d_send, d_recv, rs_send, rs_recv, ag_send, ag_recv):
     mats, tokens, rows, cols = shape
     half = rows // 2
     per = cols // W
     units = mats * per
     chunks = tokens // K
+    early = units - SPARE
+    deep = tokens // 4
     me = lax.axis_index("dp")
     core = me % 2
     bits = ((me // 8) % 2, (me // 4) % 2, (me // 2) % 2)
@@ -40,21 +44,40 @@
     def aligned(x, n):
         return pl.multiple_of(x, n)
 
-    def g_copy(i):
+    def piece(i, q):
+        return COLUMNS, pl.ds(0, deep), pl.ds(aligned((4 * lax.rem(i, 2) + q) * 2 * W, 2 * W), 2 * W)
+
+    def g_copies(i):
         n, j = i // (per // 2), lax.rem(i, per // 2)
-        return pltpu.make_async_copy(g.at[0, n, :, pl.ds(aligned(j * 2 * W, 2 * W), 2 * W)],
-                                     g_in.at[lax.rem(i, 2)], g_sem.at[lax.rem(i, 2)])
+        return [pltpu.make_async_copy(g.at[0, n, pl.ds(q * deep, deep), pl.ds(aligned(j * 2 * W, 2 * W), 2 * W)],
+                                      pool.at[piece(i, q)], g_sem.at[lax.rem(i, 2), q]) for q in range(4)]
 
     def a_copy(n, c):
-        return pltpu.make_async_copy(a.at[0, n, pl.ds(aligned(c * K, K), K), :], a_in.at[lax.rem(c, 2)], a_sem.at[lax.rem(c, 2)])
+        return pltpu.make_async_copy(a.at[0, n, pl.ds(aligned(c * K, K), K), :], a_in.at[lax.rem(c, 4)], a_sem.at[lax.rem(c, 4)])
+
+    def spot(v, row, size):
+        r = lax.rem(v, SPARE)
+        return UNITS + r // LANES, pl.ds(row, size), pl.ds(aligned(lax.rem(r, LANES) * W, W), W)
+
+    def home(v):
+        n, j = v // per, lax.rem(v, per)
+        return out.at[n, :, pl.ds(aligned(j * W, W), W)]
 
     def o_copy(v):
-        n, j = v // per, lax.rem(v, per)
-        slot = lax.rem(v, SPARE)
-        return pltpu.make_async_copy(whole.at[slot], out.at[n, :, pl.ds(aligned(j * W, W), W)], o_sem.at[lax.rem(v, 3)])
+        return pltpu.make_async_copy(pool.at[spot(v, 0, rows)], home(v), o_sem.at[lax.rem(v, 3)])
+
+    def back(f, q):
+        return pltpu.make_async_copy(home(f), pool.at[f // LANES, :, pl.ds(aligned(lax.rem(f, LANES) * W, W), W)], b_sem.at[q])
+
+    def fetch(t, act):
+        f = t - (units - per)
+        pl.when((f >= 0) & (f < LANES))(lambda: act(back(f, 0)))
+        for q in range(2):
+            f = LANES + 2 * (t - units) + q
+            pl.when((f >= LANES) & (f < early))(lambda f=f, q=q: act(back(f, q)))
 
     def flip(n, c):
-        at[lax.rem(n, 2), :, pl.ds(aligned(c * K, K), K)] = a_in[lax.rem(c, 2)].T
+        pool[lax.rem(n, 2), :, pl.ds(aligned(c * K, K), K)] = a_in[lax.rem(c, 4)].T
 
     def swap(i):
         return remote(give, take.at[lax.rem(i, 3)], d_send.at[0], d_recv.at[lax.rem(i, 3)], other)
@@ -76,12 +99,12 @@
         row, size = start_of(v, s + 1)
         _, to = route(v, s)
         q = lax.rem(v, 6)
-        ref = whole.at[lax.rem(v, SPARE), pl.ds(aligned(row, rows // 16), size), :]
+        ref = pool.at[spot(v, aligned(row, rows // 16), size)]
         return remote(ref, ref, ag_send.at[s, q], ag_recv.at[s, q], to)
 
     def share(v):
         q = lax.rem(v, 6)
-        ref = whole.at[lax.rem(v, SPARE), pl.ds(aligned(core * half, half), half), :]
+        ref = pool.at[spot(v, aligned(core * half, half), half)]
         return remote(ref, ref, ag_send.at[3, q], ag_recv.at[3, q], other)
 
     def add(v, s, mine, got, keep, send):
@@ -98,11 +121,11 @@
             pl.when((v >= 0) & (v < units))(lambda: f(v))
 
         def nine(v):
-            o_copy(v).wait()
+            pl.when(v < early)(lambda: o_copy(v).wait())
 
         def eight(v):
             share(v).wait()
-            o_copy(v).start()
+            pl.when(v < early)(lambda: o_copy(v).start())
 
         def seven(v):
             gather(v, 0).wait()
@@ -120,7 +143,7 @@
             scatter(v, 2).wait()
             row, size = start_of(v, 3)
             done = keep3[lax.rem(v, 3)] + r3[lax.rem(v, 6)].astype(jnp.float32)
-            whole[lax.rem(v, SPARE), pl.ds(aligned(row, rows // 16), size), :] = done.astype(jnp.bfloat16)
+            pool[spot(v, aligned(row, rows // 16), size)] = done.astype(jnp.bfloat16)
             gather(v, 2).start()
 
         def three(v):
@@ -145,8 +168,10 @@
         for k, f in ((9, nine), (8, eight), (7, seven), (6, six), (5, five), (4, four), (3, three), (2, two), (1, one)):
             when(k, f)
 
-    g_copy(0).start()
-    a_copy(0, 0).start()
+    for c in range(3):
+        a_copy(0, c).start()
+    for c in g_copies(0):
+        c.start()
     barrier = pltpu.get_barrier_semaphore()
     for b, bit in ((8, bits[0]), (4, bits[1]), (2, bits[2]), (1, core)):
         pl.semaphore_signal(barrier, inc=1, device_id={"dp": me + b * (1 - 2 * bit)}, device_id_type=MESH)
@@ -155,9 +180,9 @@
     def first(c, _):
         a_copy(0, c).wait()
 
-        @pl.when(c + 1 < chunks)
+        @pl.when(c + 3 < chunks)
         def _():
-            a_copy(0, c + 1).start()
+            a_copy(0, c + 3).start()
         flip(0, c)
         return 0
 
@@ -174,19 +199,24 @@
             def _():
                 a_copy(n + 1, c).start()
 
+            fetch(t - 1, lambda c: c.wait())
             stages(t, h)
+            fetch(t, lambda c: c.start())
 
             @pl.when(t < units)
             def _():
                 if h == 0:
-                    g_copy(i).wait()
+                    for c_ in g_copies(i):
+                        c_.wait()
 
                     @pl.when(i + 1 < units // 2)
                     def _():
-                        g_copy(i + 1).start()
+                        for c_ in g_copies(i + 1):
+                            c_.start()
                 side = core if h else 1 - core
-                block = jnp.dot(at[lax.rem(n, 2), pl.ds(aligned(side * half, half), half), :], g_in[lax.rem(i, 2)],
-                                preferred_element_type=jnp.float32)
+                mine = lax.rem(n, 2), pl.ds(aligned(side * half, half), half)
+                block = sum(jnp.dot(pool[(*mine, pl.ds(q * deep, deep))], pool[piece(i, q)], preferred_element_type=jnp.float32)
+                            for q in range(4))
                 if h == 0:
                     give[...] = block.astype(jnp.bfloat16)
                     swap(i).start()
@@ -200,6 +230,25 @@
         return 0
 
     lax.fori_loop(0, (units + LAG[9] + 1 + 1) // 2, pair, 0)
+
+
+def settle(shape, pool, out, sem):
+    mats, rows, cols = shape
+    per = cols // W
+    units = mats * per
+    copies, f = [], 0
+    while f < units:
+        n = min(LANES - f % LANES, per - f % per)
+        b = f // LANES if f < units - SPARE else UNITS + f % SPARE // LANES
+        for r in range(0, rows, rows // ROWS):
+            part = pl.ds(r, rows // ROWS)
+            copies.append(pltpu.make_async_copy(pool.at[b, part, pl.ds(f % LANES * W, n * W)],
+                                                out.at[f // per, part, pl.ds(f % per * W, n * W)], sem.at[len(copies)]))
+        f += n
+    for c in copies:
+        c.start()
+    for c in copies:
+        c.wait()
 
 
 def solution(mesh):
@@ -209,26 +258,31 @@
         half = rows // 2
         bf, f32 = jnp.bfloat16, jnp.float32
         dma = pltpu.SemaphoreType.DMA
-        return pl.pallas_call(
+        _, pool = pl.pallas_call(
             lambda *refs: kernel((mats, tokens, rows, cols), *refs),
-            out_shape=jax.ShapeDtypeStruct((mats, rows, cols), bf),
+            out_shape=(jax.ShapeDtypeStruct((mats, rows, cols), bf), pltpu.VMEM((BLOCKS, rows, LANES * W), bf)),
             in_specs=[pl.BlockSpec(memory_space=pl.ANY)] * 2,
-            out_specs=pl.BlockSpec(memory_space=pl.ANY),
+            out_specs=(pl.BlockSpec(memory_space=pl.ANY), pl.BlockSpec(memory_space=pltpu.VMEM)),
             scratch_shapes=[
-                pltpu.VMEM((2, rows, tokens), bf),
-                pltpu.VMEM((2, K, rows), bf),
-                pltpu.VMEM((2, tokens, 2 * W), bf),
+                pltpu.VMEM((4, K, rows), bf),
                 pltpu.VMEM((half, 2 * W), f32),
                 pltpu.VMEM((half, 2 * W), bf),
                 pltpu.VMEM((3, half, 2 * W), bf),
                 *[pltpu.VMEM((3, half // d, W), f32) for d in (2, 4, 8)],
                 *[pltpu.VMEM((3, half // d, W), bf) for d in (2, 4, 8)],
                 *[pltpu.VMEM((6, half // d, W), bf) for d in (2, 4, 8)],
-                pltpu.VMEM((SPARE, rows, W), bf),
-                dma((2,)), dma((2,)), dma((3,)), dma((1,)), dma((3,)),
+                dma((4,)), dma((2, 4)), dma((3,)), dma((2,)), dma((1,)), dma((3,)),
                 dma((3, 3)), dma((3, 6)), dma((4, 6)), dma((4, 6)),
             ],
-            compiler_params=pltpu.CompilerParams(collective_id=0, has_side_effects=True, vmem_limit_bytes=63 * 2**20),
+            compiler_params=pltpu.CompilerParams(collective_id=0, has_side_effects=True, vmem_limit_bytes=14417920),
         )(a, g)
+        return pl.pallas_call(
+            lambda *refs: settle((mats, rows, cols), *refs),
+            out_shape=jax.ShapeDtypeStruct((mats, rows, cols), bf),
+            in_specs=[pl.BlockSpec(memory_space=pltpu.VMEM)],
+            out_specs=pl.BlockSpec(memory_space=pl.ANY),
+            scratch_shapes=[dma((8 * ROWS,))],
+            compiler_params=pltpu.CompilerParams(vmem_limit_bytes=2**20),
+        )(pool)
 
     return jax.shard_map(step, mesh=mesh, in_specs=(P(("rep", "dp")), P(("rep", "dp"))), out_specs=P("rep"), check_vma=False)

time: 418 us -> 387 us (0.926)
  local copies, waits for them, and re-layouts: 35.7 us -> 0 us
  Pallas kernels: 381 us -> 387 us
    unnamed x1 -> x0, local copies, waits for them, and re-layouts: 35.7 us -> none
    pallas_call x0 -> x1, Pallas kernels: none -> 16.9 us  [step(): pl.pallas_call(lambda *refs: settle((mats, rows, cols), *refs), out_shape...]
    pallas_call x1, Pallas kernels: 381 us -> 370 us  [step(): pl.pallas_call(lambda *refs: kernel((mats, tokens, rows, cols), *refs), o...]
where the time goes in v2:
time: 387 us
  Pallas kernels  387 us (100%)
    pallas_call x1, Pallas kernels, step(): pl.pallas_call(lambda *refs: kernel((mats, tokens, rows, cols), *refs), o...  370 us
    pallas_call x1, Pallas kernels, step(): pl.pallas_call(lambda *refs: settle((mats, rows, cols), *refs), out_shape...  16.9 us

profile of v2, /device:TPU:0, one launch (start us, length us, event | category | flops | bytes accessed | tf_op | source)
XLA Modules:
  0.0 386.8 jit_solution(16449729575597205431)
XLA Ops:
  0.0 369.9 %shard_map.28 = (bf16[4,1280,5120]{2,1,0:T(8,128)(2,1)}, bf16[5,1280,4096]{2,1,0:T(8,128)(2,1)S(1)}) custom-call(bf16[1,4,4096,1280]{3,2,1,0:T(8,128)(2,1)} %refs_0_.1, bf16[1,4,4096,5120]{3,2,1,0:T(8,128)(2,1)} %refs_1_.1), custom_call_target="tpu_custom_call" | custom-call | tf_op jit(solution)/shard_map/pallas_call | solution.py:261
  369.9 16.9 %shard_map.29 = bf16[4,1280,5120]{2,1,0:T(8,128)(2,1)} custom-call(bf16[5,1280,4096]{2,1,0:T(8,128)(2,1)S(1)} %get-tuple-element.6.refs_0_), custom_call_target="tpu_custom_call" | custom-call | tf_op jit(solution)/shard_map/pallas_call | solution.py:279

commit v3 on v2

--- a/solution.py
+++ b/solution.py
@@ -70,11 +70,12 @@
         return pltpu.make_async_copy(home(f), pool.at[f // LANES, :, pl.ds(aligned(lax.rem(f, LANES) * W, W), W)], b_sem.at[q])
 
     def fetch(t, act):
+        sem = 2 * lax.rem(t, 4)
         f = t - (units - per)
-        pl.when((f >= 0) & (f < LANES))(lambda: act(back(f, 0)))
+        pl.when((f >= 0) & (f < LANES))(lambda: act(back(f, sem)))
         for q in range(2):
             f = LANES + 2 * (t - units) + q
-            pl.when((f >= LANES) & (f < early))(lambda f=f, q=q: act(back(f, q)))
+            pl.when((f >= LANES) & (f < early))(lambda f=f, q=q: act(back(f, sem + q)))
 
     def flip(n, c):
         pool[lax.rem(n, 2), :, pl.ds(aligned(c * K, K), K)] = a_in[lax.rem(c, 4)].T
@@ -98,12 +99,12 @@
     def gather(v, s):
         row, size = start_of(v, s + 1)
         _, to = route(v, s)
-        q = lax.rem(v, 6)
+        q = lax.rem(v, 12)
         ref = pool.at[spot(v, aligned(row, rows // 16), size)]
         return remote(ref, ref, ag_send.at[s, q], ag_recv.at[s, q], to)
 
     def share(v):
-        q = lax.rem(v, 6)
+        q = lax.rem(v, 12)
         ref = pool.at[spot(v, aligned(core * half, half), half)]
         return remote(ref, ref, ag_send.at[3, q], ag_recv.at[3, q], other)
 
@@ -165,7 +166,7 @@
             add(v, 0, acc.at[:, c], take.at[lax.rem(i, 3), :, c], keep1, s1)
             scatter(v, 0).start()
 
-        for k, f in ((9, nine), (8, eight), (7, seven), (6, six), (5, five), (4, four), (3, three), (2, two), (1, one)):
+        for k, f in enumerate((one, two, three, four, five, six, seven, eight, nine), 1):
             when(k, f)
 
     for c in range(3):
@@ -192,15 +193,16 @@
         n = (2 * i) // per
         for h in range(2):
             t = 2 * i + h
-            c = lax.rem(t, per)
-            ahead = (t < units - per) & (c < chunks)
+            c = 2 * (lax.rem(t, per) - (per - chunks // 2))
+            ahead = (t < units - per) & (c >= 0)
 
             @pl.when(ahead)
             def _():
                 a_copy(n + 1, c).start()
-
-            fetch(t - 1, lambda c: c.wait())
+                a_copy(n + 1, c + 1).start()
+
             stages(t, h)
+            fetch(t - 3, lambda c: c.wait())
             fetch(t, lambda c: c.start())
 
             @pl.when(t < units)
@@ -225,8 +227,9 @@
 
             @pl.when(ahead)
             def _():
-                a_copy(n + 1, c).wait()
-                flip(n + 1, c)
+                for q in range(2):
+                    a_copy(n + 1, c + q).wait()
+                    flip(n + 1, c + q)
         return 0
 
     lax.fori_loop(0, (units + LAG[9] + 1 + 1) // 2, pair, 0)
@@ -271,8 +274,8 @@
                 *[pltpu.VMEM((3, half // d, W), f32) for d in (2, 4, 8)],
                 *[pltpu.VMEM((3, half // d, W), bf) for d in (2, 4, 8)],
                 *[pltpu.VMEM((6, half // d, W), bf) for d in (2, 4, 8)],
-                dma((4,)), dma((2, 4)), dma((3,)), dma((2,)), dma((1,)), dma((3,)),
-                dma((3, 3)), dma((3, 6)), dma((4, 6)), dma((4, 6)),
+                dma((4,)), dma((2, 4)), dma((3,)), dma((8,)), dma((1,)), dma((3,)),
+                dma((3, 3)), dma((3, 6)), dma((4, 12)), dma((4, 12)),
             ],
             compiler_params=pltpu.CompilerParams(collective_id=0, has_side_effects=True, vmem_limit_bytes=14417920),
         )(a, g)

time: 387 us -> 382 us (0.987)
  Pallas kernels: 387 us -> 381 us
    pallas_call x1, Pallas kernels: 370 us -> 364 us  [step(): pl.pallas_call(lambda *refs: kernel((mats, tokens, rows, cols), *refs), o...]
where the time goes in v3:
time: 382 us; the launch traced here: 381 us
  Pallas kernels  381 us (100%)
    pallas_call x1, Pallas kernels, step(): pl.pallas_call(lambda *refs: kernel((mats, tokens, rows, cols), *refs), o...  364 us
    pallas_call x1, Pallas kernels, step(): pl.pallas_call(lambda *refs: settle((mats, rows, cols), *refs), out_shape...  16.9 us

profile of v3, /device:TPU:0, one launch (start us, length us, event | category | flops | bytes accessed | tf_op | source)
XLA Modules:
  0.0 381.3 jit_solution(16363866928258246233)
XLA Ops:
  0.0 364.4 %shard_map.28 = (bf16[4,1280,5120]{2,1,0:T(8,128)(2,1)}, bf16[5,1280,4096]{2,1,0:T(8,128)(2,1)S(1)}) custom-call(bf16[1,4,4096,1280]{3,2,1,0:T(8,128)(2,1)} %refs_0_.1, bf16[1,4,4096,5120]{3,2,1,0:T(8,128)(2,1)} %refs_1_.1), custom_call_target="tpu_custom_call" | custom-call | tf_op jit(solution)/shard_map/pallas_call | solution.py:264
  364.4 16.9 %shard_map.29 = bf16[4,1280,5120]{2,1,0:T(8,128)(2,1)} custom-call(bf16[5,1280,4096]{2,1,0:T(8,128)(2,1)S(1)} %get-tuple-element.6.refs_0_), custom_call_target="tpu_custom_call" | custom-call | tf_op jit(solution)/shard_map/pallas_call | solution.py:282

commit v4 on v3

--- a/solution.py
+++ b/solution.py
@@ -8,14 +8,14 @@
 MESH = pl.DeviceIdType.MESH
 W = 256
 K = 256
-LAG = {1: 2, 2: 4, 3: 6, 4: 8, 5: 10, 6: 13, 7: 16, 8: 18, 9: 20}
+LAG = {1: 2, 2: 4, 3: 6, 4: 8, 5: 10, 6: 13, 7: 17, 8: 19, 9: 21}
 LANES = 16
 SPARE = 2 * LANES
 COLUMNS, UNITS, BLOCKS = 2, 3, 5
 ROWS = 4
 
 def kernel(shape, a, g, out, pool, a_in, acc, give, take, keep1, keep2, keep3, s1, s2, s3, r1, r2, r3,
-           a_sem, g_sem, o_sem, b_sem, d_send, d_recv, rs_send, rs_recv, ag_send, ag_recv):
+           a_sem, f_sem, g_sem, o_sem, b_sem, d_send, d_recv, rs_send, rs_recv, ag_send, ag_recv):
     mats, tokens, rows, cols = shape
     half = rows // 2
     per = cols // W
@@ -77,6 +77,14 @@
             f = LANES + 2 * (t - units) + q
             pl.when((f >= LANES) & (f < early))(lambda f=f, q=q: act(back(f, sem + q)))
 
+    def lobby(c):
+        tall, wide = rows // K, LANES * W // rows
+        return (UNITS + c // (tall * wide), pl.ds(aligned(lax.rem(c, tall) * K, K), K),
+                pl.ds(aligned(lax.rem(c // tall, wide) * rows, rows), rows))
+
+    def a_first(c):
+        return pltpu.make_async_copy(a.at[0, 0, pl.ds(aligned(c * K, K), K), :], pool.at[lobby(c)], f_sem.at[c])
+
     def flip(n, c):
         pool[lax.rem(n, 2), :, pl.ds(aligned(c * K, K), K)] = a_in[lax.rem(c, 4)].T
 
@@ -169,8 +177,7 @@
         for k, f in enumerate((one, two, three, four, five, six, seven, eight, nine), 1):
             when(k, f)
 
-    for c in range(3):
-        a_copy(0, c).start()
+    lax.fori_loop(0, chunks, lambda c, _: (a_first(c).start(), 0)[1], 0)
     for c in g_copies(0):
         c.start()
     barrier = pltpu.get_barrier_semaphore()
@@ -179,12 +186,8 @@
     pl.semaphore_wait(barrier, 4)
 
     def first(c, _):
-        a_copy(0, c).wait()
-
-        @pl.when(c + 3 < chunks)
-        def _():
-            a_copy(0, c + 3).start()
-        flip(0, c)
+        a_first(c).wait()
+        pool[0, :, pl.ds(aligned(c * K, K), K)] = pool[lobby(c)].T
         return 0
 
     lax.fori_loop(0, chunks, first, 0)
@@ -274,7 +277,7 @@
                 *[pltpu.VMEM((3, half // d, W), f32) for d in (2, 4, 8)],
                 *[pltpu.VMEM((3, half // d, W), bf) for d in (2, 4, 8)],
                 *[pltpu.VMEM((6, half // d, W), bf) for d in (2, 4, 8)],
-                dma((4,)), dma((2, 4)), dma((3,)), dma((8,)), dma((1,)), dma((3,)),
+                dma((4,)), dma((tokens // K,)), dma((2, 4)), dma((3,)), dma((8,)), dma((1,)), dma((3,)),
                 dma((3, 3)), dma((3, 6)), dma((4, 12)), dma((4, 12)),
             ],
             compiler_params=pltpu.CompilerParams(collective_id=0, has_side_effects=True, vmem_limit_bytes=14417920),

time: 382 us -> 379 us (level)
  no operation moved by 1% of the time
where the time goes in v4:
time: 379 us; the launch traced here: 378 us
  Pallas kernels  378 us (100%)
    pallas_call x1, Pallas kernels, step(): pl.pallas_call(lambda *refs: kernel((mats, tokens, rows, cols), *refs), o...  362 us
    pallas_call x1, Pallas kernels, step(): pl.pallas_call(lambda *refs: settle((mats, rows, cols), *refs), out_shape...  16.9 us

profile of v4, /device:TPU:0, one launch (start us, length us, event | category | flops | bytes accessed | tf_op | source)
XLA Modules:
  0.0 378.5 jit_solution(4635598792334583683)
XLA Ops:
  0.0 361.6 %shard_map.28 = (bf16[4,1280,5120]{2,1,0:T(8,128)(2,1)}, bf16[5,1280,4096]{2,1,0:T(8,128)(2,1)S(1)}) custom-call(bf16[1,4,4096,1280]{3,2,1,0:T(8,128)(2,1)} %refs_0_.1, bf16[1,4,4096,5120]{3,2,1,0:T(8,128)(2,1)} %refs_1_.1), custom_call_target="tpu_custom_call" | custom-call | tf_op jit(solution)/shard_map/pallas_call | solution.py:267
  361.6 16.9 %shard_map.29 = bf16[4,1280,5120]{2,1,0:T(8,128)(2,1)} custom-call(bf16[5,1280,4096]{2,1,0:T(8,128)(2,1)S(1)} %get-tuple-element.6.refs_0_), custom_call_target="tpu_custom_call" | custom-call | tf_op jit(solution)/shard_map/pallas_call | solution.py:285
